TPU v7x, 32 devices: a whole 2x2x4 slice. The times are simulated.
32 devices in a mesh: pi: 4 (over y, x), pj: 8 (over z, core).
Axes of the slice: x: 2, y: 2, z: 4, core: 2. Of those that a mesh axis runs over, the one named last changes fastest.
Arguments:
- duo_embedding: bfloat16 [1024, 1024, 128], P('pi', 'pj'), may hold values from -12 to 12
- duo_attention_weights: float32 [128, 8], replicated, may hold values from -16 to 16
- aligned_embedding: bfloat16 [256, 64, 1024], P('pj', None, 'pi'), may hold values from -6 to 6
- aligned_scaling_weights: float32 [64], replicated, may hold values from 0.5 to 1.5
- aligned_shift_vector: float32 [64], replicated, may hold values from -3 to 3
- payload_weights: bfloat16 [64, 256], replicated, may hold values from -0.75 to 0.75
- switch_weights: bfloat16 [64, 256], replicated, may hold values from -0.75 to 0.75
- closing_weights: bfloat16 [256, 64], replicated, may hold values from -1.5 to 1.5
Outputs:
- update: bfloat16 [256, 64, 1024], P('pj', None, 'pi')
All inputs are finite; a program needn't handle non-finite values.
Results may differ from a plain program's by a relative error of at most 0.009.
Values may be sent and summed in bfloat16 or wider, within the bound.
A program may use at most 192 MiB of HBM per device.

v0:
```python
import jax
import jax.numpy as jnp
from jax import lax
from jax.sharding import PartitionSpec as P

EPS = 1e-05


def rescale_embedding(inputs, axis):
    row_mean = jnp.mean(inputs, axis=axis, keepdims=True)
    centred = inputs - row_mean
    variance = jnp.mean(centred * centred, axis=axis, keepdims=True)
    return centred * lax.rsqrt(variance + EPS)


def body(
    duo_embedding,
    duo_attention_weights,
    aligned_embedding,
    aligned_scaling_weights,
    aligned_shift_vector,
    payload_weights,
    switch_weights,
    closing_weights,
):
    attender_tally = duo_attention_weights.shape[1]
    entry_tally = duo_embedding.shape[0]
    aligned_seq_tally = aligned_embedding.shape[0]
    inner_embed_size = payload_weights.shape[1]
    attender_span = inner_embed_size // attender_tally
    pair_normed = rescale_embedding(duo_embedding.astype(jnp.float32), 2)
    scores = jnp.einsum(
        "ijc,ch->hij", pair_normed, duo_attention_weights, precision=lax.Precision.HIGHEST
    )
    row_peak = lax.pmax(jnp.max(scores, axis=2), "pj")
    exp_scores = jnp.exp(scores - row_peak[:, :, None]).astype(jnp.bfloat16)
    row_total = lax.psum(jnp.sum(exp_scores, axis=2, dtype=jnp.float32), "pj")
    weights_full = lax.all_gather(exp_scores, "pj", axis=2, tiled=True)
    rescaled_aligned = (
        rescale_embedding(aligned_embedding.astype(jnp.float32), 1)
        * aligned_scaling_weights[None, :, None]
        + aligned_shift_vector[None, :, None]
    ).astype(jnp.bfloat16)
    switch_share = jax.nn.sigmoid(
        jnp.einsum(
            "scn,ce->sen", rescaled_aligned, switch_weights, preferred_element_type=jnp.float32
        )
    )
    value_segment = jnp.einsum(
        "scn,ce->sen",
        lax.all_gather(rescaled_aligned, "pi", axis=2, tiled=True),
        payload_weights,
        preferred_element_type=jnp.float32,
    ).astype(jnp.bfloat16)
    piece_span = value_segment.shape[2]
    payload_each_attender = value_segment.reshape(
        aligned_seq_tally, attender_tally, attender_span, piece_span
    )
    numerator = jnp.einsum(
        "hij,shcj->shci", weights_full, payload_each_attender, preferred_element_type=jnp.float32
    )
    gate_per_head = switch_share.reshape(
        aligned_seq_tally, attender_tally, attender_span, entry_tally
    )
    averaged_result = (gate_per_head * (numerator / row_total[None, :, None, :])).astype(
        jnp.bfloat16
    )
    averaged_result = averaged_result.reshape(aligned_seq_tally, inner_embed_size, entry_tally)
    return jnp.einsum(
        "ser,ec->scr", averaged_result, closing_weights, preferred_element_type=jnp.float32
    ).astype(jnp.bfloat16)


def solution(mesh):
    return jax.shard_map(
        body,
        mesh=mesh,
        in_specs=(P("pi", "pj", None), P(), P("pj", None, "pi"), P(), P(), P(), P(), P()),
        out_specs=P("pj", None, "pi"),
        check_vma=False,
    )
```

profile of v0, /device:TPU:0, one launch (start us, length us, event | category | flops | bytes accessed | tf_op | source)
XLA Modules:
  0.0 166.8 jit_solution(10398905157669121667)
XLA Ops:
  6.5 0.0 copy-start
  6.5 0.0 all-gather.3.cloned.1.call-start
  6.5 1.4 convert_reduce_fusion.1
  8.0 1.6 fusion.17
  9.6 2.7 %fusion.20 = bf16[32,64,256]{2,1,0:T(8,128)(2,1)} fusion(bf16[32,64,256]{2,1,0:T(8,128)(2,1)} %param.10, f32[64]{0:T(128)} %param.12, f32[64]{0:T(128)} %param.11, f32[32,256]{1,0:T(8,128)S(1)} %add_rsqrt_fusion.1, f32[32,256]{1,0:T(8,128)S(1)} %broadcast_multiply_fusion.1), kind=kLoop, calls=%fused_computation.22 | loop fusion | flops 3145728 | bytes 2163200 | tf_op jit(solution)/shard_map/convert_element_type | solution.py:43
  12.3 0.0 all-gather.3.cloned.1.call-update
  12.4 0.0 copy-start.4
  12.4 0.0 all-gather.5.cloned.1.call-start
  12.4 0.0 slice-start
  12.4 5.8 %convert_reduce_fusion = f32[256,128]{1,0:T(8,128)S(1)} fusion(bf16[256,128,128]{2,1,0:T(8,128)(2,1)} %param.8), kind=kLoop, calls=%fused_computation.1 | loop fusion | flops 8355840 | bytes 8519680 | tf_op jit(solution)/shard_map/reduce_sum | solution.py:10
  18.3 0.0 slice-start.1
  18.3 10.9 %fusion.2 = f32[256,128]{1,0:T(8,128)S(1)} fusion(bf16[256,128,128]{2,1,0:T(8,128)(2,1)} %param.8, f32[256,128]{1,0:T(8,128)S(1)} %broadcast_multiply_fusion), kind=kLoop, calls=%fused_computation.4 | loop fusion | flops 16744448 | bytes 8650752 | tf_op jit(solution)/shard_map/reduce_sum | solution.py:12
  29.2 0.0 copy-done.4
  29.2 0.0 slice-done
  29.2 0.0 slice-done.1
  29.2 0.0 copy-start.1
  29.2 0.0 copy-start.3
  29.2 31.4 %fusion.29 = (f32[8,256]{0,1:T(8,128)S(1)}, f32[8,256,128]{2,0,1:T(8,128)S(1)}) fusion(f32[128,8]{0,1:T(8,128)S(1)} %copy-done.4, bf16[256,128,128]{2,1,0:T(8,128)(2,1)S(1)} %bitcast.34, f32[256,128]{1,0:T(8,128)S(1)} %add_rsqrt_fusion, f32[256,128]{1,0:T(8,128)S(1)} %broadcast_multiply_fusion), kind=kOutput, calls=%fused_computation.36 | convolution fusion | flops 415496192 | bytes 9711616 | tf_op jit(solution)/shard_map/ijc,ch->hij/dot_general | solution.py:32
  60.6 31.8 %pmax.7 = f32[8,256]{0,1:T(8,128)S(1)} all-reduce(f32[8,256]{0,1:T(8,128)S(1)} %get-tuple-element.7), channel_id=1, replica_groups=mesh['pi'=4,'pj'=8] {'pj'}, use_global_device_ids=true, to_apply=%region_5.0 | all-reduce | flops 2048 | bytes 16384 | tf_op jit(solution)/shard_map/pmax | solution.py:35
  92.4 1.2 convert_reduce_fusion.2
  93.6 0.0 all-gather.5.cloned.1.call-update
  93.6 30.4 %psum.7 = f32[8,256]{0,1:T(8,128)S(1)} all-reduce(f32[8,256]{0,1:T(8,128)S(1)} %get-tuple-element.5), channel_id=1, replica_groups=mesh['pi'=4,'pj'=8] {'pj'}, use_global_device_ids=true, to_apply=%region_7.0 | all-reduce | flops 2048 | bytes 16384 | tf_op jit(solution)/shard_map/psum | solution.py:37
  124.0 0.1 copy.18
  124.0 0.0 copy-done.1
  124.0 0.0 copy-done.3
  124.0 5.9 %add_divide_fusion = f32[32,256,256]{1,2,0:T(8,128)} fusion(bf16[32,64,256]{2,1,0:T(8,128)(2,1)S(1)} %copy-done.1, bf16[64,256]{1,0:T(8,128)(2,1)S(1)} %copy-done.3), kind=kOutput, calls=%fused_computation.13 | convolution fusion | flops 274726912 | bytes 9469952 | tf_op jit(solution)/shard_map/scn,ce->sen/dot_general | solution.py:45
  130.0 0.0 all-gather.3.cloned.1.call-done
  130.0 0.0 copy-done
  130.0 10.8 %convolution_convert_fusion = bf16[32,1024,256]{1,2,0:T(8,128)(2,1)} fusion(bf16[32,64,1024]{2,1,0:T(8,128)(2,1)} %all-gather.3.cloned.1.call-done, bf16[64,256]{1,0:T(8,128)(2,1)S(1)} %copy-done), kind=kOutput, calls=%fused_computation.8 | convolution fusion | flops 1082130432 | bytes 21004288 | tf_op jit(solution)/shard_map/scn,ce->sen/dot_general | solution.py:49
  140.8 0.3 all-gather.5.cloned.1.call-done
  141.1 14.4 %fusion.7 = bf16[32,8,32,256]{3,2,0,1:T(8,128)(2,1)} fusion(f32[32,8,32,256]{3,2,1,0:T(8,128)} %bitcast.38, f32[8,256]{1,0:T(8,128)S(1)} %copy.18, bf16[8,256,1024,1]{2,0,1,3:T(8,128)(2,1)} %bitcast.37, bf16[32,8,32,1024]{3,2,1,0:T(8,128)(2,1)} %bitcast.35), kind=kOutput, calls=%fused_computation.10 | convolution fusion | flops 4301258752 | bytes 33562624 | tf_op jit(solution)/shard_map/hij,shcj->shci/dot_general | solution.py:59
  155.5 0.0 copy-start.2
  155.5 2.6 %copy.20 = bf16[32,8,32,256]{3,2,1,0:T(8,128)(2,1)S(1)} copy(bf16[32,8,32,256]{3,2,0,1:T(8,128)(2,1)} %fusion.7) | data formatting | bytes 8388608 | tf_op jit(solution)/shard_map/convert_element_type | solution.py:65
  158.1 0.0 copy-done.2
  158.1 1.8 %fusion.21 = bf16[32,64,256]{2,1,0:T(8,128)(2,1)} fusion(bf16[32,256,256]{2,1,0:T(8,128)(2,1)S(1)} %bitcast.36, bf16[256,64]{0,1:T(8,128)(2,1)S(1)} %copy-done.2), kind=kOutput, calls=%fused_computation.24 | convolution fusion | flops 268959744 | bytes 5275648 | tf_op jit(solution)/shard_map/ser,ec->scr/dot_general | solution.py:69
  (5 shorter events, 0.1 us)
Async XLA Ops:
  6.5 123.4 %copy-start = (bf16[64,256]{1,0:T(8,128)(2,1)S(1)}, bf16[64,256]{1,0:T(8,128)(2,1)}, u32[]{:S(2)}) copy-start(bf16[64,256]{1,0:T(8,128)(2,1)} %param.13) | copy-start | bytes 98308
  6.5 123.4 %all-gather.3.cloned.1.call-start = ((), (), s32[]{:S(2)}) async-start(), calls=%async_computation | async-start | bytes 5242880 | tf_op jit(solution)/shard_map/all_gather | solution.py:51
  12.4 16.8 %copy-start.4 = (f32[128,8]{0,1:T(8,128)S(1)}, f32[128,8]{0,1:T(8,128)}, u32[]{:S(2)}) copy-start(f32[128,8]{0,1:T(8,128)} %param.9) | copy-start | bytes 12292
  12.4 128.7 %all-gather.5.cloned.1.call-start = ((), (), s32[]{:S(2)}) async-start(), calls=%async_computation.1 | async-start | bytes 4718592 | tf_op jit(solution)/shard_map/all_gather | solution.py:38
  12.4 16.8 %slice-start = ((s8[8388608]{0:T(1024)(128)(4,1)}), s8[4194304]{0:T(1024)(128)(4,1)S(1)}, s32[]{:S(2)}) async-start(s8[8388608]{0:T(1024)(128)(4,1)} %bitcast.33), calls=%async_computation.2 | async-start | bytes 8388608
  18.3 10.9 %slice-start.1 = ((s8[8388608]{0:T(1024)(128)(4,1)}), s8[4194304]{0:T(1024)(128)(4,1)S(1)}, s32[]{:S(2)}) async-start(s8[8388608]{0:T(1024)(128)(4,1)} %bitcast.33), calls=%async_computation.3 | async-start | bytes 8388608
  29.2 94.8 %copy-start.1 = (bf16[32,64,256]{2,1,0:T(8,128)(2,1)S(1)}, bf16[32,64,256]{2,1,0:T(8,128)(2,1)}, u32[]{:S(2)}) copy-start(bf16[32,64,256]{2,1,0:T(8,128)(2,1)} %fusion.20) | copy-start | bytes 3145732
  29.2 94.8 %copy-start.3 = (bf16[64,256]{1,0:T(8,128)(2,1)S(1)}, bf16[64,256]{1,0:T(8,128)(2,1)}, u32[]{:S(2)}) copy-start(bf16[64,256]{1,0:T(8,128)(2,1)} %param.14) | copy-start | bytes 98308
  155.5 2.6 %copy-start.2 = (bf16[256,64]{0,1:T(8,128)(2,1)S(1)}, bf16[256,64]{0,1:T(8,128)(2,1)}, u32[]{:S(2)}) copy-start(bf16[256,64]{0,1:T(8,128)(2,1)} %param.15) | copy-start | bytes 98308
Sparse Core Ops, SparseCore 0:
  12.5 55.1 all-gather.2
  93.7 47.3 all-gather.4
where the time goes:
time: 167 us
  matrix products  64.4 us (39%)
  blocking collectives  62.1 us (37%)
  other arithmetic  23.6 us (14%)
  between operations  13.6 us (8%)
  local copies, waits for them, and re-layouts  2.73 us (2%)
    pmax x1, blocking collectives, body(): row_peak = lax.pmax(jnp.max(scores, axis=2), 'pj')  31.8 us
    dot_general x1, matrix products, body(): jnp.einsum('ijc,ch->hij', pair_normed, duo_attention_weights, precision=l...  31.4 us
    psum x1, blocking collectives, body(): row_total = lax.psum(jnp.sum(exp_scores, axis=2, dtype=jnp.float32), 'pj')  30.4 us
    dot_general x1, matrix products, body(): jnp.einsum('hij,shcj->shci', weights_full, payload_each_attender, preferr...  14.4 us
    reduce_sum x2, other arithmetic, rescale_embedding(): variance = jnp.mean(centred * centred, axis=axis, keepdims=True)  12.5 us
    dot_general x1, matrix products, body(): jnp.einsum('scn,ce->sen', lax.all_gather(rescaled_aligned, 'pi', axis=2,...  10.8 us
    reduce_sum x2, other arithmetic, rescale_embedding(): row_mean = jnp.mean(inputs, axis=axis, keepdims=True)  7.24 us
    dot_general x1, matrix products, body(): jnp.einsum('scn,ce->sen', rescaled_aligned, switch_weights, preferred_ele...  5.93 us
  transfers between devices with their start and end apart: 2, of which 1 were waited for; matrix products, arithmetic and copies ran while one was open for 40% of the time, Pallas kernels for 0%

commit v1 on v0

--- a/solution.py
+++ b/solution.py
@@ -34,7 +34,9 @@
     )
     row_peak = lax.pmax(jnp.max(scores, axis=2), "pj")
     exp_scores = jnp.exp(scores - row_peak[:, :, None]).astype(jnp.bfloat16)
-    row_total = lax.psum(jnp.sum(exp_scores, axis=2, dtype=jnp.float32), "pj")
+    row_total = jnp.sum(
+        lax.all_gather(jnp.sum(exp_scores, axis=2, dtype=jnp.float32), "pj"), axis=0
+    )
     weights_full = lax.all_gather(exp_scores, "pj", axis=2, tiled=True)
     rescaled_aligned = (
         rescale_embedding(aligned_embedding.astype(jnp.float32), 1)

time: 167 us -> 166 us (level)
  blocking collectives: 62.1 us -> 46.1 us
  waiting for transfers between devices: 0.32 us -> 14.9 us
    psum x1 -> x0, blocking collectives: 30.4 us -> none  [body(): row_total = lax.psum(jnp.sum(exp_scores, axis=2, dtype=jnp.float32), 'pj')]
    all_gather x1, waiting for transfers between devices: 0.29 us -> 14.8 us  [body(): weights_full = lax.all_gather(exp_scores, 'pj', axis=2, tiled=True)]
    all_gather x0 -> x1, blocking collectives: none -> 14.4 us  [body(): lax.all_gather(jnp.sum(exp_scores, axis=2, dtype=jnp.float32), 'pj')]
where the time goes in v1:
time: 166 us; the launch traced here: 165 us
  matrix products  64.3 us (39%)
  blocking collectives  46.1 us (28%)
  other arithmetic  23.6 us (14%)
  waiting for transfers between devices  14.9 us (9%)
  between operations  13.6 us (8%)
  local copies, waits for them, and re-layouts  2.73 us (2%)
    pmax x1, blocking collectives, body(): row_peak = lax.pmax(jnp.max(scores, axis=2), 'pj')  31.8 us
    dot_general x1, matrix products, body(): jnp.einsum('ijc,ch->hij', pair_normed, duo_attention_weights, precision=l...  31.4 us
    all_gather x1, waiting for transfers between devices, body(): weights_full = lax.all_gather(exp_scores, 'pj', axis=2, tiled=True)  14.8 us
    dot_general x1, matrix products, body(): jnp.einsum('hij,shcj->shci', weights_full, payload_each_attender, preferr...  14.4 us
    all_gather x1, blocking collectives, body(): lax.all_gather(jnp.sum(exp_scores, axis=2, dtype=jnp.float32), 'pj')  14.4 us
    reduce_sum x2, other arithmetic, rescale_embedding(): variance = jnp.mean(centred * centred, axis=axis, keepdims=True)  12.5 us
    dot_general x1, matrix products, body(): jnp.einsum('scn,ce->sen', lax.all_gather(rescaled_aligned, 'pi', axis=2,...  10.8 us
    reduce_sum x2, other arithmetic, rescale_embedding(): row_mean = jnp.mean(inputs, axis=axis, keepdims=True)  7.24 us
  transfers between devices with their start and end apart: 2, of which 1 were waited for; matrix products, arithmetic and copies ran while one was open for 40% of the time, Pallas kernels for 0%

profile of v1, /device:TPU:0, one launch (start us, length us, event | category | flops | bytes accessed | tf_op | source)
XLA Modules:
  0.0 165.3 jit_solution(1883269506123242119)
XLA Ops:
  6.5 0.0 copy-start
  6.5 0.0 all-gather.4.cloned.1.call-start
  6.5 1.4 convert_reduce_fusion.1
  8.0 1.6 fusion.17
  9.6 2.7 %fusion.20 = bf16[32,64,256]{2,1,0:T(8,128)(2,1)} fusion(bf16[32,64,256]{2,1,0:T(8,128)(2,1)} %param.10, f32[64]{0:T(128)} %param.12, f32[64]{0:T(128)} %param.11, f32[32,256]{1,0:T(8,128)S(1)} %add_rsqrt_fusion.1, f32[32,256]{1,0:T(8,128)S(1)} %broadcast_multiply_fusion.1), kind=kLoop, calls=%fused_computation.22 | loop fusion | flops 3145728 | bytes 2163200 | tf_op jit(solution)/shard_map/convert_element_type | solution.py:45
  12.3 0.0 all-gather.4.cloned.1.call-update
  12.4 0.0 copy-start.4
  12.4 0.0 all-gather.6.cloned.1.call-start
  12.4 0.0 slice-start
  12.4 5.8 %convert_reduce_fusion = f32[256,128]{1,0:T(8,128)S(1)} fusion(bf16[256,128,128]{2,1,0:T(8,128)(2,1)} %param.8), kind=kLoop, calls=%fused_computation.1 | loop fusion | flops 8355840 | bytes 8519680 | tf_op jit(solution)/shard_map/reduce_sum | solution.py:10
  18.3 0.0 slice-start.1
  18.3 10.9 %fusion.2 = f32[256,128]{1,0:T(8,128)S(1)} fusion(bf16[256,128,128]{2,1,0:T(8,128)(2,1)} %param.8, f32[256,128]{1,0:T(8,128)S(1)} %broadcast_multiply_fusion), kind=kLoop, calls=%fused_computation.4 | loop fusion | flops 16744448 | bytes 8650752 | tf_op jit(solution)/shard_map/reduce_sum | solution.py:12
  29.2 0.0 copy-done.4
  29.2 0.0 slice-done
  29.2 0.0 slice-done.1
  29.2 0.0 copy-start.1
  29.2 0.0 copy-start.3
  29.2 31.4 %fusion.29 = (f32[8,256]{0,1:T(8,128)S(1)}, f32[8,256,128]{2,0,1:T(8,128)S(1)}) fusion(f32[128,8]{0,1:T(8,128)S(1)} %copy-done.4, bf16[256,128,128]{2,1,0:T(8,128)(2,1)S(1)} %bitcast.36, f32[256,128]{1,0:T(8,128)S(1)} %add_rsqrt_fusion, f32[256,128]{1,0:T(8,128)S(1)} %broadcast_multiply_fusion), kind=kOutput, calls=%fused_computation.37 | convolution fusion | flops 415496192 | bytes 9711616 | tf_op jit(solution)/shard_map/ijc,ch->hij/dot_general | solution.py:32
  60.6 31.8 %pmax.7 = f32[8,256]{0,1:T(8,128)S(1)} all-reduce(f32[8,256]{0,1:T(8,128)S(1)} %get-tuple-element.7), channel_id=1, replica_groups=mesh['pi'=4,'pj'=8] {'pj'}, use_global_device_ids=true, to_apply=%region_5.0 | all-reduce | flops 2048 | bytes 16384 | tf_op jit(solution)/shard_map/pmax | solution.py:35
  92.4 1.2 convert_reduce_fusion.2
  93.6 0.0 all-gather.6.cloned.1.call-update
  93.6 0.1 copy.27
  93.6 14.4 %all-gather = f32[64,256]{1,0:T(8,128)S(1)} all-gather(f32[8,256]{1,0:T(8,128)S(1)} %copy.27), channel_id=2, replica_groups=mesh['pi'=4,'pj'=8] {'pj'}, dimensions={0}, use_global_device_ids=true | all-gather | bytes 73728 | tf_op jit(solution)/shard_map/all_gather | solution.py:38
  108.0 0.0 copy-done.1
  108.0 0.0 copy-done.3
  108.0 5.9 %add_divide_fusion = f32[32,256,256]{1,2,0:T(8,128)} fusion(bf16[32,64,256]{2,1,0:T(8,128)(2,1)S(1)} %copy-done.1, bf16[64,256]{1,0:T(8,128)(2,1)S(1)} %copy-done.3), kind=kOutput, calls=%fused_computation.13 | convolution fusion | flops 274726912 | bytes 9469952 | tf_op jit(solution)/shard_map/scn,ce->sen/dot_general | solution.py:47
  114.0 0.0 all-gather.4.cloned.1.call-done
  114.0 0.0 copy-done
  114.0 10.8 %convolution_convert_fusion = bf16[32,1024,256]{1,2,0:T(8,128)(2,1)} fusion(bf16[32,64,1024]{2,1,0:T(8,128)(2,1)} %all-gather.4.cloned.1.call-done, bf16[64,256]{1,0:T(8,128)(2,1)S(1)} %copy-done), kind=kOutput, calls=%fused_computation.8 | convolution fusion | flops 1082130432 | bytes 21004288 | tf_op jit(solution)/shard_map/scn,ce->sen/dot_general | solution.py:51
  124.8 14.8 %all-gather.6.cloned.1.call-done = bf16[8,256,1024]{2,0,1:T(8,128)(2,1)} async-done(((bf16[8,256,128]{2,0,1:T(8,128)(2,1)}), bf16[8,256,1024]{2,0,1:T(8,128)(2,1)}) %all-gather.6.cloned.1.call-update) | async-done | bytes 4194320 | tf_op jit(solution)/shard_map/all_gather | solution.py:40
  139.6 14.4 %fusion.7 = bf16[32,8,32,256]{3,2,0,1:T(8,128)(2,1)} fusion(f32[32,8,32,256]{3,2,1,0:T(8,128)} %bitcast.40, f32[8,256]{1,0:T(8,128)S(1)} %bitcast_reduce_fusion, bf16[8,256,1024,1]{2,0,1,3:T(8,128)(2,1)} %bitcast.39, bf16[32,8,32,1024]{3,2,1,0:T(8,128)(2,1)} %bitcast.37), kind=kOutput, calls=%fused_computation.10 | convolution fusion | flops 4301258752 | bytes 33562624 | tf_op jit(solution)/shard_map/hij,shcj->shci/dot_general | solution.py:61
  154.0 0.0 copy-start.2
  154.0 2.6 %copy.29 = bf16[32,8,32,256]{3,2,1,0:T(8,128)(2,1)S(1)} copy(bf16[32,8,32,256]{3,2,0,1:T(8,128)(2,1)} %fusion.7) | data formatting | bytes 8388608 | tf_op jit(solution)/shard_map/convert_element_type | solution.py:67
  156.6 0.0 copy-done.2
  156.7 1.8 %fusion.21 = bf16[32,64,256]{2,1,0:T(8,128)(2,1)} fusion(bf16[32,256,256]{2,1,0:T(8,128)(2,1)S(1)} %bitcast.38, bf16[256,64]{0,1:T(8,128)(2,1)S(1)} %copy-done.2), kind=kOutput, calls=%fused_computation.24 | convolution fusion | flops 268959744 | bytes 5275648 | tf_op jit(solution)/shard_map/ser,ec->scr/dot_general | solution.py:71
  (6 shorter events, 0.1 us)
Async XLA Ops:
  6.5 107.4 %copy-start = (bf16[64,256]{1,0:T(8,128)(2,1)S(1)}, bf16[64,256]{1,0:T(8,128)(2,1)}, u32[]{:S(2)}) copy-start(bf16[64,256]{1,0:T(8,128)(2,1)} %param.13) | copy-start | bytes 98308
  6.5 107.4 %all-gather.4.cloned.1.call-start = ((), (), s32[]{:S(2)}) async-start(), calls=%async_computation | async-start | bytes 5242880 | tf_op jit(solution)/shard_map/all_gather | solution.py:53
  12.4 16.8 %copy-start.4 = (f32[128,8]{0,1:T(8,128)S(1)}, f32[128,8]{0,1:T(8,128)}, u32[]{:S(2)}) copy-start(f32[128,8]{0,1:T(8,128)} %param.9) | copy-start | bytes 12292
  12.4 127.2 %all-gather.6.cloned.1.call-start = ((), (), s32[]{:S(2)}) async-start(), calls=%async_computation.1 | async-start | bytes 4718592 | tf_op jit(solution)/shard_map/all_gather | solution.py:40
  12.4 16.8 %slice-start = ((s8[8388608]{0:T(1024)(128)(4,1)}), s8[4194304]{0:T(1024)(128)(4,1)S(1)}, s32[]{:S(2)}) async-start(s8[8388608]{0:T(1024)(128)(4,1)} %bitcast.35), calls=%async_computation.2 | async-start | bytes 8388608
  18.3 10.9 %slice-start.1 = ((s8[8388608]{0:T(1024)(128)(4,1)}), s8[4194304]{0:T(1024)(128)(4,1)S(1)}, s32[]{:S(2)}) async-start(s8[8388608]{0:T(1024)(128)(4,1)} %bitcast.35), calls=%async_computation.3 | async-start | bytes 8388608
  29.2 78.8 %copy-start.1 = (bf16[32,64,256]{2,1,0:T(8,128)(2,1)S(1)}, bf16[32,64,256]{2,1,0:T(8,128)(2,1)}, u32[]{:S(2)}) copy-start(bf16[32,64,256]{2,1,0:T(8,128)(2,1)} %fusion.20) | copy-start | bytes 3145732
  29.2 78.8 %copy-start.3 = (bf16[64,256]{1,0:T(8,128)(2,1)S(1)}, bf16[64,256]{1,0:T(8,128)(2,1)}, u32[]{:S(2)}) copy-start(bf16[64,256]{1,0:T(8,128)(2,1)} %param.14) | copy-start | bytes 98308
  154.0 2.6 %copy-start.2 = (bf16[256,64]{0,1:T(8,128)(2,1)S(1)}, bf16[256,64]{0,1:T(8,128)(2,1)}, u32[]{:S(2)}) copy-start(bf16[256,64]{0,1:T(8,128)(2,1)} %param.15) | copy-start | bytes 98308
Sparse Core Ops, SparseCore 0:
  12.5 55.1 all-gather.3
  93.7 45.8 all-gather.5
